TPU v7x, 32 devices: a whole 2x2x4 slice. The times are simulated.
32 devices in a mesh: tm: 8 (over z, x), tp: 4 (over y, core).
Axes of the slice: x: 2, y: 2, z: 4, core: 2. Of those that a mesh axis runs over, the one named last changes fastest.
Arguments:
- trajectory: float32 [16, 128, 3072], P('tm', None, 'tp'), may hold values from -6 to 6
- offset: int32 [1], replicated, may hold values from 0 to 15
- step_gaps: int32 [16], P('tm'), may hold values from 1 to 4, as said below
- qkv_weight: bfloat16 [3072, 3, 3072], P(None, None, 'tp')
- out_weight: bfloat16 [3072, 3072], P('tp'), may hold values from -4 to 4
- mod_weight: bfloat16 [256, 3, 3072], P(None, None, 'tp'), may hold values from -0.375 to 0.375
Outputs:
- advanced: float32 [16, 128, 3072], P('tm', None, 'tp')
Inputs may be any that keep to these rules, and one draw needn't show every extreme that they name: `step_gaps`: in aligned blocks of 2 timesteps, the gaps of block b sum to an even number for even b and to an odd number for odd b.
All inputs are finite; a program needn't handle non-finite values.
Results may differ from a plain program's by a relative error of at most 0.007.
Values may be sent and summed in bfloat16 or wider, within the bound.
A program may use at most 128 MiB of HBM per device.

v0:
```python
import math
import jax
import jax.numpy as jnp
from jax import lax
from jax.sharding import PartitionSpec as P

HD = 128
FREQ = 256
ITERS = 2


def prefix(array, axis, combine, identity):
    size, place = (lax.axis_size(axis), lax.axis_index(axis))
    everything = lax.all_gather(array, axis)
    start = jnp.broadcast_to(jnp.asarray(identity, array.dtype), array.shape)

    def turn(k, before):
        reached = k < place
        new = combine(before, everything[k])
        return jnp.where(reached, new, before)

    return lax.fori_loop(0, size, turn, start)


def prefix_2(array, axis, join, neutral):
    place = lax.axis_index(axis)
    gathered = lax.all_gather(array.astype(jnp.bfloat16), axis)
    state = jnp.zeros_like(array) + jnp.asarray(neutral, array.dtype)

    def one(turn, state):
        return join(state, lax.dynamic_index_in_dim(gathered, turn, 0, False).astype(array.dtype))

    return lax.fori_loop(0, place, one, state)


def add_up(earlier, later):
    return earlier + later


def embedding(sigma):
    half_freq = FREQ // 2
    frequencies = jnp.exp(-math.log(10000.0) * jnp.arange(half_freq, dtype=jnp.float32) / half_freq)
    angles = 1000.0 * sigma[:, None] * frequencies[None, :]
    return jnp.concatenate([jnp.cos(angles), jnp.sin(angles)], -1).astype(jnp.bfloat16)


def body(trajectory, offset, step_gaps, qkv_weight, out_weight, mod_weight):
    steps_here, tok_count, col_count = trajectory.shape
    full_width = qkv_weight.shape[0]
    time_count = steps_here * lax.axis_size("tm")
    level_count = 5 * time_count
    before = prefix(jnp.sum(step_gaps), "tm", add_up, jnp.int32(0))
    levels = (offset[0] + before + jnp.cumsum(step_gaps) - step_gaps).astype(jnp.float32)
    sigma = 1.0 - levels / level_count
    step_size = step_gaps.astype(jnp.float32) / level_count
    embed_rows = embedding(sigma)
    full_mod = lax.all_gather(mod_weight, "tp", axis=2, tiled=True)
    modulation = jnp.dot(
        embed_rows, full_mod.reshape(FREQ, 3 * full_width), preferred_element_type=jnp.float32
    ).reshape(steps_here, 3, full_width)
    gate_rows = lax.dynamic_slice_in_dim(
        modulation[:, 2], lax.axis_index("tp") * col_count, col_count, 1
    )
    first_point = jnp.where(lax.axis_index("tm") == 0, trajectory[0], jnp.zeros_like(trajectory[0]))
    flat_qkv = qkv_weight.reshape(full_width, -1)
    states = trajectory
    points = trajectory
    for sweep in range(ITERS):
        whole_rows = lax.all_gather(states, "tp", axis=2, tiled=True)
        row_mean = jnp.sum(whole_rows, -1, keepdims=True) / full_width
        variance = (
            jnp.sum(whole_rows * whole_rows, -1, keepdims=True) / full_width - row_mean * row_mean
        )
        inv_std = lax.rsqrt(variance + 1e-06)
        normed = (
            (whole_rows - row_mean) * inv_std * (1.0 + modulation[:, 1][:, None, :])
            + modulation[:, 0][:, None, :]
        ).astype(jnp.bfloat16)
        projected = jnp.einsum("std,de->ste", normed, flat_qkv, preferred_element_type=jnp.float32)
        projected = projected.astype(jnp.bfloat16).reshape(steps_here, tok_count, 3, -1, HD)
        queries = projected[:, :, 0]
        key_rows = projected[:, :, 1]
        values = projected[:, :, 2]
        scores = jnp.einsum(
            "sqhd,skhd->shqk", queries, key_rows, preferred_element_type=jnp.float32
        ) * (1.0 / math.sqrt(HD))
        row_max = jnp.max(scores, -1, keepdims=True)
        weights_exp = jnp.exp(scores - row_max)
        probs = (weights_exp / jnp.sum(weights_exp, -1, keepdims=True)).astype(jnp.bfloat16)
        attended = jnp.einsum(
            "shqk,skhd->sqhd", probs, values, preferred_element_type=jnp.float32
        ).astype(jnp.bfloat16)
        attended = attended.reshape(steps_here, tok_count, -1)
        head_out = jnp.einsum(
            "sqe,ed->sqd", attended, out_weight, preferred_element_type=jnp.float32
        )
        col_share = lax.psum_scatter(
            head_out.astype(jnp.bfloat16), "tp", scatter_dimension=2, tiled=True
        ).astype(jnp.float32)
        drifts = gate_rows[:, None, :] * col_share
        increments = -step_size[:, None, None] * drifts
        local_cum = jnp.cumsum(increments, 0)
        prefix_sum = prefix_2(
            local_cum[-1] + first_point,
            "tm",
            add_up,
            jnp.zeros((tok_count, col_count), jnp.float32),
        )
        entry_point = prefix_sum + first_point
        points = entry_point[None] + local_cum
        states = jnp.concatenate([entry_point[None], points[:-1]], 0)
    return points


def solution(mesh):
    placed = (
        P("tm", None, "tp"),
        P(),
        P("tm"),
        P(None, None, "tp"),
        P("tp", None),
        P(None, None, "tp"),
    )
    return jax.shard_map(
        body, mesh=mesh, in_specs=placed, out_specs=P("tm", None, "tp"), check_vma=False
    )
```

profile of v0, /device:TPU:26, one launch (start us, length us, event | category | flops | bytes accessed | tf_op | source)
XLA Modules:
  0.0 313.7 jit_solution(12103827058173000939)
XLA Ops:
  6.5 0.7 all-gather.8.cloned.1.call-update
  7.3 2.4 copy.33
  9.8 0.7 dynamic-slice.1
  10.5 0.6 reduce_sum.63
  11.1 1.4 dynamic-update-slice
  12.6 8.2 %all-reduce = s32[8]{0:T(128)S(1)} all-reduce(s32[8]{0:T(128)S(1)} %dynamic-update-slice), channel_id=1, replica_groups=mesh['tm'=8,'tp'=4] {'tm'}, use_global_device_ids=true, to_apply=%add | all-reduce | flops 8 | bytes 64
  21.6 18.7 %copy.34 = bf16[3072,3,768]{0,2,1:T(8,128)(2,1)} copy(bf16[3072,3,768]{2,0,1:T(8,128)(2,1)} %param.15) | data formatting | bytes 28311552 | tf_op args[3]
  40.3 10.1 %while.33 = (s32[]{:T(128)}, s32[]{:T(128)}, s32[]{:T(128)}, s32[8]{0:T(128)S(1)}, s32[]{:T(128)}) while((s32[]{:T(128)}, s32[]{:T(128)}, s32[]{:T(128)}, s32[8]{0:T(128)S(1)}, s32[]{:T(128)}) %tuple.62), condition=%wide.region_2.3_spmd, body=%wide.region_1.2_spmd.sunk | while | flops 5 | bytes 107 | solution.py:22
  41.6 0.6 dynamic_slice.24
  42.8 0.6 dynamic_slice.24
  44.1 0.6 dynamic_slice.24
  50.6 2.4 fusion.57
  53.1 24.4 %all-gather.6.cloned.1.call-done = bf16[256,3,3072]{0,2,1:T(8,128)(2,1)} async-done(((bf16[256,3,768]{0,2,1:T(8,128)(2,1)}), bf16[256,3,3072]{0,2,1:T(8,128)(2,1)}) %all-gather.6.cloned.1.call-update) | async-done | bytes 4718608 | tf_op jit(solution)/shard_map/all_gather | solution.py:57
  77.4 3.6 %fusion.2 = f32[2,3,3072]{2,0,1:T(2,128)S(1)} fusion(bf16[256,3,3072]{0,2,1:T(8,128)(2,1)} %all-gather.6.cloned.1.call-done, bf16[2,128]{1,0:T(2,128)(2,1)S(1)} %get-tuple-element.169, bf16[2,128]{1,0:T(2,128)(2,1)S(1)} %get-tuple-element.168), kind=kOutput, calls=%fused_computation.4 | convolution fusion | flops 9439232 | bytes 4793344 | tf_op jit(solution)/shard_map/dot_general | solution.py:58
  81.1 10.0 %convolution_convert_fusion.1 = bf16[2,128,2304]{2,1,0:T(8,128)(2,1)S(1)} fusion(bf16[3072,2304,1]{0,1,2:T(8,128)(2,1)} %bitcast.117, f32[2,128,3072]{2,1,0:T(8,128)} %all-gather.8.cloned.1.call-done, f32[2,3072]{1,0:T(2,128)S(1)} %get-tuple-element.162, f32[2,3072]{1,0:T(2,128)S(1)} %get-tuple-element.163, f32[2,128]{1,0:T(2,128)S(1)} %get-tuple-element.167, ...), kind=kOutput, calls=%fused_computation.13 | convolution fusion | flops 3628400640 | bytes 18532352 | tf_op jit(solution)/shard_map/std,de->ste/dot_general | solution.py:79
  91.1 0.7 copy.36
  93.0 5.0 %fusion.8 = bf16[2,128,3072]{2,1,0:T(8,128)(2,1)} fusion(bf16[2,128,768]{1,2,0:T(8,128)(2,1)S(1)} %bitcast.126, bf16[768,3072]{1,0:T(8,128)(2,1)} %param.16), kind=kOutput, calls=%fused_computation.10 | convolution fusion | flops 1208745984 | bytes 6684672 | tf_op jit(solution)/shard_map/sqe,ed->sqd/dot_general | solution.py:94
  98.1 28.1 %reduce-scatter.3.cloned.1.call-done = bf16[2,128,768]{2,1,0:T(8,128)(2,1)} async-done(((bf16[2,128,3072]{2,1,0:T(8,128)(2,1)}), bf16[2,128,768]{2,1,0:T(8,128)(2,1)}) %reduce-scatter.3.cloned.1.call-update) | async-done | bytes 393232 | tf_op jit(solution)/shard_map/reduce_scatter | solution.py:97
  126.2 1.1 fusion.30
  127.3 0.7 fusion.35
  128.1 41.8 %all-gather.10.cloned.1.call-done = bf16[8,128,768]{2,1,0:T(8,128)(2,1)} async-done(((bf16[1,128,768]{2,1,0:T(8,128)(2,1)}), bf16[8,128,768]{2,1,0:T(8,128)(2,1)}) %all-gather.10.cloned.1.call-update) | async-done | bytes 1572880 | tf_op jit(solution)/shard_map/all_gather | solution.py:27
  169.9 7.2 %while.34 = (s32[]{:T(128)}, f32[128,768]{1,0:T(8,128)S(1)}, s32[]{:T(128)}, bf16[8,128,768]{2,1,0:T(8,128)(2,1)}, s32[]{:T(128)}, /*index=5*/s32[]{:T(128)}, s32[]{:T(128)}) while((s32[]{:T(128)}, f32[128,768]{1,0:T(8,128)S(1)}, s32[]{:T(128)}, bf16[8,128,768]{2,1,0:T(8,128)(2,1)}, s32[]{:T(128)}, /*index=5*/s32[]{:T(128)}, ...), condition=%wide.region_11.12_spmd, body=%wide.region_10.11_spmd.sunk | while | flops 196613 | bytes 983155 | solution.py:33
  170.0 1.0 convert_add_fusion.4
  171.0 1.0 convert_add_fusion.4
  172.0 1.0 convert_add_fusion.4
  173.1 1.0 convert_add_fusion.4
  174.1 1.0 convert_add_fusion.4
  175.1 1.0 convert_add_fusion.4
  176.1 1.0 convert_add_fusion.4
  177.3 0.9 pad_maximum_fusion
  178.5 29.3 %all-gather.12.cloned.1.call-done = f32[2,128,3072]{2,1,0:T(8,128)} async-done(((f32[2,128,768]{2,1,0:T(8,128)}), f32[2,128,3072]{2,1,0:T(8,128)}) %all-gather.12.cloned.1.call-update) | async-done | bytes 3145744 | tf_op jit(solution)/shard_map/all_gather | solution.py:69
  207.8 2.6 fusion.56
  210.6 9.2 %convolution_convert_fusion = bf16[2,128,2304]{2,1,0:T(8,128)(2,1)S(1)} fusion(bf16[3072,2304,1]{0,1,2:T(8,128)(2,1)} %bitcast.118, f32[2,128,3072]{2,1,0:T(8,128)S(1)} %copy-done.1, f32[2,128]{1,0:T(2,128)S(1)} %get-tuple-element.165, f32[2,128]{1,0:T(2,128)S(1)} %get-tuple-element.164, f32[2,3072]{1,0:T(2,128)} %copy-done.2, f32[2,3072]{1,0:T(2,128)} %copy-done.3), kind=kOutput, calls=%fused_computation.12 | convolution fusion | flops 3628400640 | bytes 18532352 | tf_op jit(solution)/shard_map/std,de->ste/dot_general | solution.py:79
  219.8 0.7 copy.43
  221.7 4.9 %fusion.11 = bf16[2,128,3072]{2,1,0:T(8,128)(2,1)} fusion(bf16[2,128,768]{1,2,0:T(8,128)(2,1)S(1)} %bitcast.127, bf16[768,3072]{1,0:T(8,128)(2,1)} %param.16), kind=kOutput, calls=%fused_computation.11 | convolution fusion | flops 1208745984 | bytes 6684672 | tf_op jit(solution)/shard_map/sqe,ed->sqd/dot_general | solution.py:94
  226.6 28.1 %reduce-scatter.5.cloned.1.call-done = bf16[2,128,768]{2,1,0:T(8,128)(2,1)} async-done(((bf16[2,128,3072]{2,1,0:T(8,128)(2,1)}), bf16[2,128,768]{2,1,0:T(8,128)(2,1)}) %reduce-scatter.5.cloned.1.call-update) | async-done | bytes 393232 | tf_op jit(solution)/shard_map/reduce_scatter | solution.py:97
  254.8 1.1 fusion.26
  255.9 0.7 fusion.34
  256.6 42.0 %all-gather.14.cloned.1.call-done = bf16[8,128,768]{2,1,0:T(8,128)(2,1)} async-done(((bf16[1,128,768]{2,1,0:T(8,128)(2,1)}), bf16[8,128,768]{2,1,0:T(8,128)(2,1)}) %all-gather.14.cloned.1.call-update) | async-done | bytes 1572880 | tf_op jit(solution)/shard_map/all_gather | solution.py:27
  298.6 7.2 %while.35 = (s32[]{:T(128)}, f32[128,768]{1,0:T(8,128)S(1)}, s32[]{:T(128)}, bf16[8,128,768]{2,1,0:T(8,128)(2,1)}, s32[]{:T(128)}, /*index=5*/s32[]{:T(128)}, s32[]{:T(128)}) while((s32[]{:T(128)}, f32[128,768]{1,0:T(8,128)S(1)}, s32[]{:T(128)}, bf16[8,128,768]{2,1,0:T(8,128)(2,1)}, s32[]{:T(128)}, /*index=5*/s32[]{:T(128)}, ...), condition=%wide.region_19.20_spmd, body=%wide.region_18.19_spmd.sunk | while | flops 196613 | bytes 983155 | solution.py:33
  298.7 1.0 convert_add_fusion.5
  299.7 1.0 convert_add_fusion.5
  300.7 1.0 convert_add_fusion.5
  301.7 1.0 convert_add_fusion.5
  302.8 1.0 convert_add_fusion.5
  303.8 1.0 convert_add_fusion.5
  304.8 1.0 convert_add_fusion.5
  305.9 0.9 broadcast_add_fusion
  (51 shorter events, 6.6 us)
Async XLA Ops:
  6.5 3.3 %copy-start.5 = (u32[32]{0:T(128)S(1)}, u32[32]{0:T(128)}, u32[]{:S(2)}) copy-start(u32[32]{0:T(128)} %constant.91) | copy-start | bytes 388
  6.5 3.9 %copy-start.4 = (s32[2]{0:T(128)S(1)}, s32[2]{0:T(128)}, u32[]{:S(2)}) copy-start(s32[2]{0:T(128)} %param.14) | copy-start | bytes 28
  6.5 44.1 %all-gather.8.cloned.1.call-start = ((), (), s32[]{:S(2)}) async-start(), calls=%async_computation.3 | async-start | bytes 3932160 | tf_op jit(solution)/shard_map/all_gather | solution.py:69
  7.3 70.2 %all-gather.6.cloned.1.call-start = ((), (), s32[]{:S(2)}) async-start(), calls=%async_computation.2 | async-start | bytes 5898240 | tf_op jit(solution)/shard_map/all_gather | solution.py:57
  9.7 116.5 %reduce-scatter.3.cloned.1.call-start = ((), (), s32[]{:S(2)}) async-start(), calls=%async_computation.4 | async-start | bytes 1966080 | tf_op jit(solution)/shard_map/reduce_scatter | solution.py:97
  81.1 10.0 %copy-start.2 = (f32[2,3072]{1,0:T(2,128)}, f32[2,3072]{1,0:T(2,128)S(1)}, u32[]{:S(2)}) copy-start(f32[2,3072]{1,0:T(2,128)S(1)} %get-tuple-element.162) | copy-start | bytes 73732
  81.1 10.0 %copy-start.3 = (f32[2,3072]{1,0:T(2,128)}, f32[2,3072]{1,0:T(2,128)S(1)}, u32[]{:S(2)}) copy-start(f32[2,3072]{1,0:T(2,128)S(1)} %get-tuple-element.163) | copy-start | bytes 73732
  93.0 34.3 %copy-start = (f32[2,128,768]{2,1,0:T(8,128)S(1)}, f32[2,128,768]{2,1,0:T(8,128)}, u32[]{:S(2)}) copy-start(f32[2,128,768]{2,1,0:T(8,128)} %param.12) | copy-start | bytes 2359300
  98.0 71.9 %all-gather.10.cloned.1.call-start = ((), (), s32[]{:S(2)}) async-start(), calls=%async_computation.5 | async-start | bytes 1769472 | tf_op jit(solution)/shard_map/all_gather | solution.py:27
  128.1 79.7 %all-gather.12.cloned.1.call-start = ((), (), s32[]{:S(2)}) async-start(), calls=%async_computation.6 | async-start | bytes 3932160 | tf_op jit(solution)/shard_map/all_gather | solution.py:69
  178.2 76.5 %reduce-scatter.5.cloned.1.call-start = ((), (), s32[]{:S(2)}) async-start(), calls=%async_computation.7 | async-start | bytes 1966080 | tf_op jit(solution)/shard_map/reduce_scatter | solution.py:97
  207.8 2.8 copy-start.1
  226.6 72.0 %all-gather.14.cloned.1.call-start = ((), (), s32[]{:S(2)}) async-start(), calls=%async_computation.8 | async-start | bytes 1769472 | tf_op jit(solution)/shard_map/all_gather | solution.py:27
Sparse Core Ops, SparseCore 0:
  8.9 29.4 all-gather.7
  40.0 37.4 all-gather.5
  98.1 28.0 reduce-scatter.2
  128.3 41.6 all-gather.9
  178.3 29.4 all-gather.11
  226.7 28.0 reduce-scatter.4
  256.9 41.6 all-gather.13
where the time goes:
time: 315 us; the launch traced here: 314 us
  waiting for transfers between devices  195 us (62%)
  matrix products  34.9 us (11%)
  local copies, waits for them, and re-layouts  29.8 us (9%)
  other arithmetic  25.7 us (8%)
  between operations  14.4 us (5%)
  blocking collectives  8.23 us (3%)
  loops' own time  5.66 us (2%)
    all_gather x2, waiting for transfers between devices, prefix_2(): gathered = lax.all_gather(array.astype(jnp.bfloat16), axis)  83.7 us
    reduce_scatter x2, waiting for transfers between devices, body(): lax.psum_scatter(head_out.astype(jnp.bfloat16), 'tp', scatter_dimension=2...  56.3 us
    all_gather x2, waiting for transfers between devices, body(): whole_rows = lax.all_gather(states, 'tp', axis=2, tiled=True)  29.4 us
    all_gather x1, waiting for transfers between devices, body(): full_mod = lax.all_gather(mod_weight, 'tp', axis=2, tiled=True)  24.4 us
    unnamed x17, local copies, waits for them, and re-layouts  23.4 us
    dot_general x2, matrix products, body(): jnp.einsum('std,de->ste', normed, flat_qkv, preferred_element_type=jnp.fl...  19.1 us
    add x14, other arithmetic, add_up(): return earlier + later  14 us
    dot_general x2, matrix products, body(): jnp.einsum('sqe,ed->sqd', attended, out_weight, preferred_element_type=jn...  9.87 us
  transfers between devices with their start and end apart: 7, of which 6 were waited for; matrix products, arithmetic and copies ran while one was open for 10% of the time, Pallas kernels for 0%

commit v1 on v0

--- a/solution.py
+++ b/solution.py
@@ -54,7 +54,12 @@
     sigma = 1.0 - levels / level_count
     step_size = step_gaps.astype(jnp.float32) / level_count
     embed_rows = embedding(sigma)
-    full_mod = lax.all_gather(mod_weight, "tp", axis=2, tiled=True)
+    ring = [mod_weight]
+    for hop in range(3):
+        ring.append(lax.ppermute(ring[-1], "tp", [(dev, (dev + 1) % 4) for dev in range(4)]))
+    full_mod = jnp.roll(
+        jnp.concatenate(ring[::-1], axis=2), (lax.axis_index("tp") + 1) * ring[0].shape[2], axis=2
+    )
     modulation = jnp.dot(
         embed_rows, full_mod.reshape(FREQ, 3 * full_width), preferred_element_type=jnp.float32
     ).reshape(steps_here, 3, full_width)

time: 315 us -> 337 us (1.070)
  waiting for transfers between devices: 195 us -> 215 us
    ppermute x0 -> x3, waiting for transfers between devices: none -> 43.9 us  [body(): lax.ppermute(ring[-1], 'tp', [(dev, (dev + 1) % 4) for dev in range(4)])]
    all_gather x1 -> x0, waiting for transfers between devices: 24.4 us -> none  [body(): full_mod = lax.all_gather(mod_weight, 'tp', axis=2, tiled=True)]
    unnamed x17 -> x28, local copies, waits for them, and re-layouts: 23.4 us -> 25.7 us
  transfers between devices with their start and end apart: 7 -> 9, of which waited for: 6 -> 7; matrix products, arithmetic and copies ran while one was open for 10% -> 9% of each run, Pallas kernels for 0% -> 0%
where the time goes in v1:
time: 337 us; the launch traced here: 336 us
  waiting for transfers between devices  215 us (64%)
  local copies, waits for them, and re-layouts  32.6 us (10%)
  matrix products  32.6 us (10%)
  other arithmetic  25.7 us (8%)
  between operations  14.5 us (4%)
  blocking collectives  8.23 us (2%)
  loops' own time  6.1 us (2%)
    all_gather x2, waiting for transfers between devices, prefix_2(): gathered = lax.all_gather(array.astype(jnp.bfloat16), axis)  83.8 us
    reduce_scatter x2, waiting for transfers between devices, body(): lax.psum_scatter(head_out.astype(jnp.bfloat16), 'tp', scatter_dimension=2...  57.5 us
    ppermute x3, waiting for transfers between devices, body(): lax.ppermute(ring[-1], 'tp', [(dev, (dev + 1) % 4) for dev in range(4)])  43.9 us
    all_gather x2, waiting for transfers between devices, body(): whole_rows = lax.all_gather(states, 'tp', axis=2, tiled=True)  29.4 us
    unnamed x28, local copies, waits for them, and re-layouts  25.7 us
    dot_general x2, matrix products, body(): jnp.einsum('std,de->ste', normed, flat_qkv, preferred_element_type=jnp.fl...  19.1 us
    add x14, other arithmetic, add_up(): return earlier + later  14 us
    dot_general x2, matrix products, body(): jnp.einsum('sqe,ed->sqd', attended, out_weight, preferred_element_type=jn...  9.87 us
  transfers between devices with their start and end apart: 9, of which 7 were waited for; matrix products, arithmetic and copies ran while one was open for 9% of the time, Pallas kernels for 0%

profile of v1, /device:TPU:26, one launch (start us, length us, event | category | flops | bytes accessed | tf_op | source)
XLA Modules:
  0.0 335.9 jit_solution(13405608998375497594)
XLA Ops:
  6.5 1.6 copy.35
  8.3 23.1 %collective-permute-done = bf16[256,3,768]{0,2,1:T(8,128)(2,1)S(1)} collective-permute-done((bf16[256,3,768]{0,2,1:T(8,128)(2,1)S(1)}, bf16[256,3,768]{0,2,1:T(8,128)(2,1)S(1)}, u32[]{:S(2)}, u32[]{:S(2)}) %collective-permute-start) | collective-permute-done | bytes 1179680 | tf_op jit(solution)/shard_map/ppermute | solution.py:59
  31.4 1.1 collective-permute-start.1
  32.5 20.8 %collective-permute-done.1 = bf16[256,3,768]{0,2,1:T(8,128)(2,1)S(1)} collective-permute-done((bf16[256,3,768]{0,2,1:T(8,128)(2,1)S(1)}, bf16[256,3,768]{0,2,1:T(8,128)(2,1)S(1)}, u32[]{:S(2)}, u32[]{:S(2)}) %collective-permute-start.1) | collective-permute-done | bytes 1179680 | tf_op jit(solution)/shard_map/ppermute | solution.py:59
  54.6 1.4 dynamic-update-slice
  56.1 8.2 %all-reduce = s32[8]{0:T(128)S(1)} all-reduce(s32[8]{0:T(128)S(1)} %dynamic-update-slice), channel_id=1, replica_groups=mesh['tm'=8,'tp'=4] {'tm'}, use_global_device_ids=true, to_apply=%add | all-reduce | flops 8 | bytes 64
  65.1 18.6 %copy.38 = bf16[3072,3,768]{0,2,1:T(8,128)(2,1)} copy(bf16[3072,3,768]{2,0,1:T(8,128)(2,1)} %param.15) | data formatting | bytes 28311552 | tf_op args[3]
  83.8 11.0 %while.33 = (s32[]{:T(128)}, s32[]{:T(128)}, s32[]{:T(128)}, s32[8]{0:T(128)S(1)}, s32[]{:T(128)}) while((s32[]{:T(128)}, s32[]{:T(128)}, s32[]{:T(128)}, s32[8]{0:T(128)S(1)}, s32[]{:T(128)}) %tuple.62), condition=%wide.region_2.3_spmd, body=%wide.region_1.2_spmd.sunk | while | flops 5 | bytes 107 | solution.py:22
  85.1 0.7 dynamic_slice.33
  86.5 0.7 dynamic_slice.33
  95.0 1.3 constant_dynamic-update-slice_fusion.7
  96.6 1.3 constant_dynamic-update-slice_fusion.3
  98.2 1.3 fusion.2
  99.6 2.6 fusion.59
  102.4 9.1 %convolution_convert_fusion.1 = bf16[2,128,2304]{2,1,0:T(8,128)(2,1)S(1)} fusion(bf16[3072,2304,1]{0,1,2:T(8,128)(2,1)} %bitcast.117, f32[2,128,3072]{2,1,0:T(8,128)S(1)} %copy-done.1, f32[2,3072]{1,0:T(2,128)S(1)} %get-tuple-element.162, f32[2,3072]{1,0:T(2,128)S(1)} %get-tuple-element.163, f32[2,128]{1,0:T(2,128)S(1)} %get-tuple-element.167, ...), kind=kOutput, calls=%fused_computation.14 | convolution fusion | flops 3628400640 | bytes 18532352 | tf_op jit(solution)/shard_map/std,de->ste/dot_general | solution.py:84
  111.6 0.7 copy.40
  113.5 5.0 %fusion.9 = bf16[2,128,3072]{2,1,0:T(8,128)(2,1)} fusion(bf16[2,128,768]{1,2,0:T(8,128)(2,1)S(1)} %bitcast.126, bf16[768,3072]{1,0:T(8,128)(2,1)} %param.16), kind=kOutput, calls=%fused_computation.11 | convolution fusion | flops 1208745984 | bytes 6684672 | tf_op jit(solution)/shard_map/sqe,ed->sqd/dot_general | solution.py:99
  118.5 29.4 %reduce-scatter.3.cloned.1.call-done = bf16[2,128,768]{2,1,0:T(8,128)(2,1)} async-done(((bf16[2,128,3072]{2,1,0:T(8,128)(2,1)}), bf16[2,128,768]{2,1,0:T(8,128)(2,1)}) %reduce-scatter.3.cloned.1.call-update) | async-done | bytes 393232 | tf_op jit(solution)/shard_map/reduce_scatter | solution.py:102
  147.9 1.1 fusion.31
  149.1 0.7 fusion.36
  149.9 41.9 %all-gather.7.cloned.1.call-done = bf16[8,128,768]{2,1,0:T(8,128)(2,1)} async-done(((bf16[1,128,768]{2,1,0:T(8,128)(2,1)}), bf16[8,128,768]{2,1,0:T(8,128)(2,1)}) %all-gather.7.cloned.1.call-update) | async-done | bytes 1572880 | tf_op jit(solution)/shard_map/all_gather | solution.py:27
  191.8 7.2 %while.34 = (s32[]{:T(128)}, f32[128,768]{1,0:T(8,128)S(1)}, s32[]{:T(128)}, bf16[8,128,768]{2,1,0:T(8,128)(2,1)}, s32[]{:T(128)}, /*index=5*/s32[]{:T(128)}, s32[]{:T(128)}) while((s32[]{:T(128)}, f32[128,768]{1,0:T(8,128)S(1)}, s32[]{:T(128)}, bf16[8,128,768]{2,1,0:T(8,128)(2,1)}, s32[]{:T(128)}, /*index=5*/s32[]{:T(128)}, ...), condition=%wide.region_11.12_spmd, body=%wide.region_10.11_spmd.sunk | while | flops 196613 | bytes 983155 | solution.py:33
  191.8 1.0 convert_add_fusion.4
  192.9 1.0 convert_add_fusion.4
  193.9 1.0 convert_add_fusion.4
  194.9 1.0 convert_add_fusion.4
  196.0 1.0 convert_add_fusion.4
  197.0 1.0 convert_add_fusion.4
  198.0 1.0 convert_add_fusion.4
  199.2 0.9 pad_maximum_fusion
  200.3 29.3 %all-gather.9.cloned.1.call-done = f32[2,128,3072]{2,1,0:T(8,128)} async-done(((f32[2,128,768]{2,1,0:T(8,128)}), f32[2,128,3072]{2,1,0:T(8,128)}) %all-gather.9.cloned.1.call-update) | async-done | bytes 3145744 | tf_op jit(solution)/shard_map/all_gather | solution.py:74
  229.7 2.4 fusion.58
  232.2 10.0 %convolution_convert_fusion = bf16[2,128,2304]{2,1,0:T(8,128)(2,1)S(1)} fusion(bf16[3072,2304,1]{0,1,2:T(8,128)(2,1)} %bitcast.118, f32[2,128,3072]{2,1,0:T(8,128)} %all-gather.9.cloned.1.call-done, f32[2,128]{1,0:T(2,128)S(1)} %get-tuple-element.165, f32[2,128]{1,0:T(2,128)S(1)} %get-tuple-element.164, f32[2,3072]{1,0:T(2,128)S(1)} %copy-done.3, ...), kind=kOutput, calls=%fused_computation.13 | convolution fusion | flops 3628400640 | bytes 18532352 | tf_op jit(solution)/shard_map/std,de->ste/dot_general | solution.py:84
  242.2 0.7 copy.47
  244.0 4.9 %fusion.12 = bf16[2,128,3072]{2,1,0:T(8,128)(2,1)} fusion(bf16[2,128,768]{1,2,0:T(8,128)(2,1)S(1)} %bitcast.127, bf16[768,3072]{1,0:T(8,128)(2,1)} %param.16), kind=kOutput, calls=%fused_computation.12 | convolution fusion | flops 1208745984 | bytes 6684672 | tf_op jit(solution)/shard_map/sqe,ed->sqd/dot_general | solution.py:99
  249.0 28.1 %reduce-scatter.5.cloned.1.call-done = bf16[2,128,768]{2,1,0:T(8,128)(2,1)} async-done(((bf16[2,128,3072]{2,1,0:T(8,128)(2,1)}), bf16[2,128,768]{2,1,0:T(8,128)(2,1)}) %reduce-scatter.5.cloned.1.call-update) | async-done | bytes 393232 | tf_op jit(solution)/shard_map/reduce_scatter | solution.py:102
  277.1 1.1 fusion.27
  278.2 0.7 fusion.35
  279.0 41.8 %all-gather.11.cloned.1.call-done = bf16[8,128,768]{2,1,0:T(8,128)(2,1)} async-done(((bf16[1,128,768]{2,1,0:T(8,128)(2,1)}), bf16[8,128,768]{2,1,0:T(8,128)(2,1)}) %all-gather.11.cloned.1.call-update) | async-done | bytes 1572880 | tf_op jit(solution)/shard_map/all_gather | solution.py:27
  320.9 7.2 %while.35 = (s32[]{:T(128)}, f32[128,768]{1,0:T(8,128)S(1)}, s32[]{:T(128)}, bf16[8,128,768]{2,1,0:T(8,128)(2,1)}, s32[]{:T(128)}, /*index=5*/s32[]{:T(128)}, s32[]{:T(128)}) while((s32[]{:T(128)}, f32[128,768]{1,0:T(8,128)S(1)}, s32[]{:T(128)}, bf16[8,128,768]{2,1,0:T(8,128)(2,1)}, s32[]{:T(128)}, /*index=5*/s32[]{:T(128)}, ...), condition=%wide.region_19.20_spmd, body=%wide.region_18.19_spmd.sunk | while | flops 196613 | bytes 983155 | solution.py:33
  320.9 1.0 convert_add_fusion.5
  321.9 1.0 convert_add_fusion.5
  322.9 1.0 convert_add_fusion.5
  324.0 1.0 convert_add_fusion.5
  325.0 1.0 convert_add_fusion.5
  326.0 1.0 convert_add_fusion.5
  327.1 1.0 convert_add_fusion.5
  328.1 0.9 broadcast_add_fusion
  (66 shorter events, 9.4 us)
Async XLA Ops:
  6.5 46.8 %copy-start.7 = (u32[32]{0:T(128)S(1)}, u32[32]{0:T(128)}, u32[]{:S(2)}) copy-start(u32[32]{0:T(128)} %constant.110) | copy-start | bytes 388
  6.5 47.4 %copy-start.6 = (s32[2]{0:T(128)S(1)}, s32[2]{0:T(128)}, u32[]{:S(2)}) copy-start(s32[2]{0:T(128)} %param.14) | copy-start | bytes 28
  6.5 93.0 %all-gather.5.cloned.1.call-start = ((), (), s32[]{:S(2)}) async-start(), calls=%async_computation.2 | async-start | bytes 3932160 | tf_op jit(solution)/shard_map/all_gather | solution.py:74
  8.1 23.2 %collective-permute-start = (bf16[256,3,768]{0,2,1:T(8,128)(2,1)S(1)}, bf16[256,3,768]{0,2,1:T(8,128)(2,1)S(1)}, u32[]{:S(2)}, u32[]{:S(2)}) collective-permute-start(bf16[256,3,768]{0,2,1:T(8,128)(2,1)S(1)} %copy.35), channel_id=1, source_target_pairs={{0,1},{1,2},{2,3},{3,0},{4,5},{5,6},{6,7},{7,4},{8,9},{9,10},{10,1... | collective-permute-start | bytes 3538952 | tf_op jit(solution)/shard_map/ppermute | solution.py:59
  8.2 139.7 %reduce-scatter.3.cloned.1.call-start = ((), (), s32[]{:S(2)}) async-start(), calls=%async_computation.3 | async-start | bytes 1966080 | tf_op jit(solution)/shard_map/reduce_scatter | solution.py:102
  31.4 21.9 %collective-permute-start.1 = (bf16[256,3,768]{0,2,1:T(8,128)(2,1)S(1)}, bf16[256,3,768]{0,2,1:T(8,128)(2,1)S(1)}, u32[]{:S(2)}, u32[]{:S(2)}) collective-permute-start(bf16[256,3,768]{0,2,1:T(8,128)(2,1)S(1)} %collective-permute-done), channel_id=1, source_target_pairs={{0,1},{1,2},{2,3},{3,0},{4,5},{5,6},{6,7},{7,4},{8,9},{9,10},{10,1... | collective-permute-start | bytes 3538952 | tf_op jit(solution)/shard_map/ppermute | solution.py:59
  53.3 41.6 %collective-permute-start.2 = (bf16[256,3,768]{0,2,1:T(8,128)(2,1)S(1)}, bf16[256,3,768]{0,2,1:T(8,128)(2,1)}, u32[]{:S(2)}, u32[]{:S(2)}) collective-permute-start(bf16[256,3,768]{0,2,1:T(8,128)(2,1)S(1)} %collective-permute-done.1), channel_id=1, source_target_pairs={{0,1},{1,2},{2,3},{3,0},{4,5},{5,6},{6,7},{7,4},{8,9},{9,10},{10,1... | collective-permute-start | bytes 3538952 | tf_op jit(solution)/shard_map/ppermute | solution.py:59
  99.5 12.0 %copy-start.2 = (f32[2,3072]{1,0:T(2,128)}, f32[2,3072]{1,0:T(2,128)S(1)}, u32[]{:S(2)}) copy-start(f32[2,3072]{1,0:T(2,128)S(1)} %get-tuple-element.162) | copy-start | bytes 73732
  99.6 12.0 %copy-start.4 = (f32[2,3072]{1,0:T(2,128)}, f32[2,3072]{1,0:T(2,128)S(1)}, u32[]{:S(2)}) copy-start(f32[2,3072]{1,0:T(2,128)S(1)} %get-tuple-element.163) | copy-start | bytes 73732
  99.6 2.8 copy-start.1
  113.4 35.6 %copy-start = (f32[2,128,768]{2,1,0:T(8,128)S(1)}, f32[2,128,768]{2,1,0:T(8,128)}, u32[]{:S(2)}) copy-start(f32[2,128,768]{2,1,0:T(8,128)} %param.12) | copy-start | bytes 2359300
  118.4 73.3 %all-gather.7.cloned.1.call-start = ((), (), s32[]{:S(2)}) async-start(), calls=%async_computation.4 | async-start | bytes 1769472 | tf_op jit(solution)/shard_map/all_gather | solution.py:27
  149.8 79.9 %all-gather.9.cloned.1.call-start = ((), (), s32[]{:S(2)}) async-start(), calls=%async_computation.5 | async-start | bytes 3932160 | tf_op jit(solution)/shard_map/all_gather | solution.py:74
  199.1 33.1 %copy-start.3 = (f32[2,3072]{1,0:T(2,128)S(1)}, f32[2,3072]{1,0:T(2,128)}, u32[]{:S(2)}) copy-start(f32[2,3072]{1,0:T(2,128)} %copy-done.2) | copy-start | bytes 73732
  199.1 33.1 %copy-start.5 = (f32[2,3072]{1,0:T(2,128)S(1)}, f32[2,3072]{1,0:T(2,128)}, u32[]{:S(2)}) copy-start(f32[2,3072]{1,0:T(2,128)} %copy-done.4) | copy-start | bytes 73732
  200.1 77.0 %reduce-scatter.5.cloned.1.call-start = ((), (), s32[]{:S(2)}) async-start(), calls=%async_computation.6 | async-start | bytes 1966080 | tf_op jit(solution)/shard_map/reduce_scatter | solution.py:102
  249.0 71.9 %all-gather.11.cloned.1.call-start = ((), (), s32[]{:S(2)}) async-start(), calls=%async_computation.7 | async-start | bytes 1769472 | tf_op jit(solution)/shard_map/all_gather | solution.py:27
Sparse Core Ops, SparseCore 0:
  8.9 36.4 all-gather.4
  118.6 29.3 reduce-scatter.2
  150.1 41.6 all-gather.6
  200.2 29.4 all-gather.8
  249.1 27.9 reduce-scatter.4
  279.2 41.6 all-gather.10
